TPU v7x, 32 devices: a whole 2x2x4 slice. The times are simulated.
32 devices in a mesh: row: 8 (over y, x, core), col: 4 (over z).
Axes of the slice: x: 2, y: 2, z: 4, core: 2. Of those that a mesh axis runs over, the one named last changes fastest.
Arguments:
- jacobian: float32 [2, 4096, 256], P(None, ('row', 'col')), may hold values from -0.25 to 0.25
Outputs:
- normal_tiles: float32 [8, 2, 4, 512, 512], P('row', None, 'col')
All inputs are finite; a program needn't handle non-finite values.
Results may differ from a plain program's by a relative error of at most 0.0003.
Values sent between devices are 32-bit elements; how exact they have to be, the bound alone decides.
A program may use at most 64 MiB of HBM per device.

v0:
```python
import jax
import jax.numpy as jnp
from jax import lax
from jax.sharding import PartitionSpec as P


def from_partner(block, axis, distance):
    count = lax.axis_size(axis)
    route = []
    for low in range(count):
        high = low | 1 << distance
        if high != low and high < count:
            route += [(low, high), (high, low)]
    return lax.ppermute(block, axis, route)


def partner_rows(block, bit_number):
    return from_partner(block, ("row", "col"), bit_number)


def body(jacobian):
    row_index = lax.axis_index("row")
    col_index = lax.axis_index("col")
    col_count = lax.axis_size("col")
    cycles = lax.axis_size("row") // col_count
    panel_count = jacobian.shape[0]
    width = jacobian.shape[2]
    own_tile = lax.all_gather(jacobian, "col", axis=1, tiled=True)
    tile_size = own_tile.shape[1]
    col_bits = col_count.bit_length() - 1
    low_row = row_index % col_count
    moved = jacobian
    for bit_number in range(col_bits):
        first = partner_rows(moved, bit_number)
        second = partner_rows(first, bit_number + col_bits)
        differ = low_row >> bit_number & 1 != col_index >> bit_number & 1
        moved = jnp.where(differ, second, moved)
    gathered = lax.all_gather(moved, "row", axis=1, tiled=True)
    gathered = gathered.reshape(panel_count, cycles, tile_size, width)
    partners = [gathered[:, turn_index] for turn_index in range(cycles)]

    def product(partner):
        return jnp.einsum("pak,pbk->ab", own_tile, partner, precision=lax.Precision.HIGHEST)

    def empty_tile(partner):
        return jnp.zeros((tile_size, tile_size), jnp.float32)

    results = []
    for turn_index in range(cycles):
        column_tile = col_index + col_count * turn_index
        results.append(
            lax.cond(column_tile <= row_index, product, empty_tile, partners[turn_index])
        )
    blocks = jnp.stack(results, 0)
    return blocks[None, :, None]


def solution(mesh):
    in_specs = (P(None, ("row", "col"), None),)
    out_specs = P("row", None, "col", None, None)
    return jax.shard_map(body, mesh=mesh, in_specs=in_specs, out_specs=out_specs, check_vma=False)
```

profile of v0, /device:TPU:4, one launch (start us, length us, event | category | flops | bytes accessed | tf_op | source)
XLA Modules:
  0.0 115.7 jit_solution(6772489944896085306)
XLA Ops:
  6.5 0.0 all-gather.3.cloned.1.call-start
  6.5 1.6 %collective-permute-start = (f32[2,128,256]{2,1,0:T(8,128)}, f32[2,128,256]{2,1,0:T(8,128)S(1)}, u32[]{:S(2)}, u32[]{:S(2)}) collective-permute-start(f32[2,128,256]{2,1,0:T(8,128)} %param.5), channel_id=1, source_target_pairs={{0,1},{1,0},{2,3},{3,2},{4,5},{5,4},{6,7},{7,6},{8,9},{9,8},{10,11... | collective-permute-start | bytes 786440 | tf_op jit(solution)/shard_map/ppermute | solution.py:14
  8.1 6.7 %collective-permute-done = f32[2,128,256]{2,1,0:T(8,128)S(1)} collective-permute-done((f32[2,128,256]{2,1,0:T(8,128)}, f32[2,128,256]{2,1,0:T(8,128)S(1)}, u32[]{:S(2)}, u32[]{:S(2)}) %collective-permute-start) | collective-permute-done | bytes 262176 | tf_op jit(solution)/shard_map/ppermute | solution.py:14
  14.8 0.0 collective-permute-start.1
  14.8 1.5 %collective-permute-done.1 = f32[2,128,256]{2,1,0:T(8,128)S(1)} collective-permute-done((f32[2,128,256]{2,1,0:T(8,128)S(1)}, f32[2,128,256]{2,1,0:T(8,128)S(1)}, u32[]{:S(2)}, u32[]{:S(2)}) %collective-permute-start.1) | collective-permute-done | bytes 262176 | tf_op jit(solution)/shard_map/ppermute | solution.py:14
  16.3 1.0 broadcast_select_fusion
  17.3 2.7 %collective-permute-start.2 = (f32[2,128,256]{2,1,0:T(8,128)S(1)}, f32[2,128,256]{2,1,0:T(8,128)S(1)}, u32[]{:S(2)}, u32[]{:S(2)}) collective-permute-start(f32[2,128,256]{2,1,0:T(8,128)S(1)} %broadcast_select_fusion), channel_id=1, source_target_pairs={{0,2},{2,0},{1,3},{3,1},{4,6},{6,4},{5,7},{7,5},{8,10},{10,8},{9,1... | collective-permute-start | bytes 786440 | tf_op jit(solution)/shard_map/ppermute | solution.py:14
  20.0 11.3 %collective-permute-done.2 = f32[2,128,256]{2,1,0:T(8,128)S(1)} collective-permute-done((f32[2,128,256]{2,1,0:T(8,128)S(1)}, f32[2,128,256]{2,1,0:T(8,128)S(1)}, u32[]{:S(2)}, u32[]{:S(2)}) %collective-permute-start.2) | collective-permute-done | bytes 262176 | tf_op jit(solution)/shard_map/ppermute | solution.py:14
  31.3 1.5 %collective-permute-start.3 = (f32[2,128,256]{2,1,0:T(8,128)S(1)}, f32[2,128,256]{2,1,0:T(8,128)S(1)}, u32[]{:S(2)}, u32[]{:S(2)}) collective-permute-start(f32[2,128,256]{2,1,0:T(8,128)S(1)} %collective-permute-done.2), channel_id=1, source_target_pairs={{0,8},{8,0},{1,9},{9,1},{2,10},{10,2},{3,11},{11,3},{4,12},{12,4},... | collective-permute-start | bytes 786440 | tf_op jit(solution)/shard_map/ppermute | solution.py:14
  32.8 5.1 %collective-permute-done.3 = f32[2,128,256]{2,1,0:T(8,128)S(1)} collective-permute-done((f32[2,128,256]{2,1,0:T(8,128)S(1)}, f32[2,128,256]{2,1,0:T(8,128)S(1)}, u32[]{:S(2)}, u32[]{:S(2)}) %collective-permute-start.3) | collective-permute-done | bytes 262176 | tf_op jit(solution)/shard_map/ppermute | solution.py:14
  37.8 0.7 broadcast_select_fusion.1
  38.6 0.0 all-gather.3.cloned.1.call-update
  38.6 0.0 all-gather.5.cloned.1.call-start
  38.7 0.7 all-gather.5.cloned.1.call-update
  39.4 30.0 %all-gather.3.cloned.1.call-done = f32[2,1024,256]{2,1,0:T(8,128)} async-done(((f32[2,128,256]{2,1,0:T(8,128)}), f32[2,1024,256]{2,1,0:T(8,128)}) %all-gather.3.cloned.1.call-update) | async-done | bytes 2097168 | tf_op jit(solution)/shard_map/all_gather | solution.py:38
  69.3 1.7 %copy.2 = f32[2,2,512,256]{3,2,0,1:T(8,128)S(1)} copy(f32[2,2,512,256]{3,2,1,0:T(8,128)} %bitcast.17) | data formatting | bytes 4194304 | tf_op jit(solution)/shard_map/cond | solution.py:52
  71.1 27.9 %all-gather.5.cloned.1.call-done = f32[2,512,256]{2,1,0:T(8,128)} async-done(((f32[2,128,256]{2,1,0:T(8,128)}), f32[2,512,256]{2,1,0:T(8,128)}) %all-gather.5.cloned.1.call-update) | async-done | bytes 1048592 | tf_op jit(solution)/shard_map/all_gather | solution.py:28
  99.0 3.1 %conditional.3 = (f32[1,512,512]{2,1,0:T(8,128)S(1)}) conditional(s32[]{:T(128)} %convert_element_type.7, () %tuple.23, (f32[2,2,512,256]{3,2,0,1:T(8,128)S(1)}, f32[2,512,256]{2,1,0:T(8,128)}) %tuple.24), branch_computations={%region_2.3_spmd, %region_3.4_spmd} | conditional | flops 1610612736 | bytes 3145736 | solution.py:52
  99.0 3.1 %convolution_bitcast_fusion.1 = f32[1,512,512]{2,1,0:T(8,128)S(1)} fusion(f32[2,512,256]{2,1,0:T(8,128)} %get-tuple-element.27, f32[2,2,512,256]{3,2,0,1:T(8,128)S(1)} %get-tuple-element.28), kind=kOutput, calls=%fused_computation.3 | convolution fusion | flops 1610612736 | bytes 3145728 | tf_op jit(solution)/shard_map/cond/branch_1_fun/pak,pbk->ab/dot_general | solution.py:43
  102.1 4.1 %conditional.2 = (f32[1,512,512]{2,1,0:T(8,128)}) conditional(s32[]{:T(128)} %convert_element_type.6, () %tuple.21, (f32[2,2,512,256]{3,2,0,1:T(8,128)S(1)}, f32[2,512,256]{2,1,0:T(8,128)}) %tuple.24), branch_computations={%region_0.1_spmd, %region_1.2_spmd} | conditional | flops 1610612736 | bytes 3145736 | solution.py:52
  102.1 4.1 %convolution_bitcast_fusion = f32[1,512,512]{2,1,0:T(8,128)} fusion(f32[2,512,256]{2,1,0:T(8,128)} %get-tuple-element.25, f32[2,2,512,256]{3,2,0,1:T(8,128)S(1)} %get-tuple-element.26), kind=kOutput, calls=%fused_computation | convolution fusion | flops 1610612736 | bytes 3145728 | tf_op jit(solution)/shard_map/cond/branch_1_fun/pak,pbk->ab/dot_general | solution.py:43
  106.2 2.7 %maximum_bitcast_fusion = f32[1,2,1,512,512]{4,3,2,1,0:T(8,128)} fusion(f32[1,512,512]{2,1,0:T(8,128)S(1)} %get-tuple-element.34, f32[1,512,512]{2,1,0:T(8,128)} %get-tuple-element.33), kind=kLoop, calls=%fused_computation.6 | loop fusion | flops 524288 | bytes 4194304 | tf_op jit(solution)/shard_map/broadcast_in_dim | solution.py:55
Async XLA Ops:
  6.5 62.8 %all-gather.3.cloned.1.call-start = ((), (), s32[]{:S(2)}) async-start(), calls=%async_computation | async-start | bytes 2359296 | tf_op jit(solution)/shard_map/all_gather | solution.py:38
  6.5 8.3 %collective-permute-start = (f32[2,128,256]{2,1,0:T(8,128)}, f32[2,128,256]{2,1,0:T(8,128)S(1)}, u32[]{:S(2)}, u32[]{:S(2)}) collective-permute-start(f32[2,128,256]{2,1,0:T(8,128)} %param.5), channel_id=1, source_target_pairs={{0,1},{1,0},{2,3},{3,2},{4,5},{5,4},{6,7},{7,6},{8,9},{9,8},{10,11... | collective-permute-start | bytes 786440 | tf_op jit(solution)/shard_map/ppermute | solution.py:14
  14.8 1.5 %collective-permute-start.1 = (f32[2,128,256]{2,1,0:T(8,128)S(1)}, f32[2,128,256]{2,1,0:T(8,128)S(1)}, u32[]{:S(2)}, u32[]{:S(2)}) collective-permute-start(f32[2,128,256]{2,1,0:T(8,128)S(1)} %collective-permute-done), channel_id=1, source_target_pairs={{0,4},{4,0},{1,5},{5,1},{2,6},{6,2},{3,7},{7,3},{8,12},{12,8},{9,1... | collective-permute-start | bytes 786440 | tf_op jit(solution)/shard_map/ppermute | solution.py:14
  17.3 14.0 %collective-permute-start.2 = (f32[2,128,256]{2,1,0:T(8,128)S(1)}, f32[2,128,256]{2,1,0:T(8,128)S(1)}, u32[]{:S(2)}, u32[]{:S(2)}) collective-permute-start(f32[2,128,256]{2,1,0:T(8,128)S(1)} %broadcast_select_fusion), channel_id=1, source_target_pairs={{0,2},{2,0},{1,3},{3,1},{4,6},{6,4},{5,7},{7,5},{8,10},{10,8},{9,1... | collective-permute-start | bytes 786440 | tf_op jit(solution)/shard_map/ppermute | solution.py:14
  31.3 6.5 %collective-permute-start.3 = (f32[2,128,256]{2,1,0:T(8,128)S(1)}, f32[2,128,256]{2,1,0:T(8,128)S(1)}, u32[]{:S(2)}, u32[]{:S(2)}) collective-permute-start(f32[2,128,256]{2,1,0:T(8,128)S(1)} %collective-permute-done.2), channel_id=1, source_target_pairs={{0,8},{8,0},{1,9},{9,1},{2,10},{10,2},{3,11},{11,3},{4,12},{12,4},... | collective-permute-start | bytes 786440 | tf_op jit(solution)/shard_map/ppermute | solution.py:14
  38.6 60.4 %all-gather.5.cloned.1.call-start = ((), (), s32[]{:S(2)}) async-start(), calls=%async_computation.1 | async-start | bytes 1310720 | tf_op jit(solution)/shard_map/all_gather | solution.py:28
Sparse Core Ops, SparseCore 0:
  38.7 30.5 all-gather.2
  70.9 28.0 all-gather.4
where the time goes:
time: 116 us
  waiting for transfers between devices  83.2 us (72%)
  between operations  13.4 us (12%)
  matrix products  7.14 us (6%)
  starting transfers between devices  5.77 us (5%)
  other arithmetic  4.43 us (4%)
  local copies, waits for them, and re-layouts  1.73 us (1%)
    all_gather x1, waiting for transfers between devices, body(): gathered = lax.all_gather(moved, 'row', axis=1, tiled=True)  30 us
    all_gather x1, waiting for transfers between devices, body(): own_tile = lax.all_gather(jacobian, 'col', axis=1, tiled=True)  27.9 us
    ppermute x4, waiting for transfers between devices, from_partner(): return lax.ppermute(block, axis, route)  24.6 us
    dot_general x2, matrix products, product(): jnp.einsum('pak,pbk->ab', own_tile, partner, precision=lax.Precision.HIGH...  7.14 us
    ppermute x4, starting transfers between devices, from_partner(): return lax.ppermute(block, axis, route)  5.72 us
    broadcast_in_dim x1, other arithmetic, body(): return blocks[None, :, None]  2.71 us
  transfers between devices with their start and end apart: 6, of which 6 were waited for; matrix products, arithmetic and copies ran while one was open for 1% of the time, Pallas kernels for 0%

commit v1 on v0

--- a/solution.py
+++ b/solution.py
@@ -35,7 +35,17 @@
         second = partner_rows(first, bit_number + col_bits)
         differ = low_row >> bit_number & 1 != col_index >> bit_number & 1
         moved = jnp.where(differ, second, moved)
-    gathered = lax.all_gather(moved, "row", axis=1, tiled=True)
+    nd = jax.lax.axis_size("row")
+    arr_next = sorted(((jj, (jj + 1) % nd) for jj in range(nd)))
+    o_now = moved
+    runs = [o_now]
+    for t in range(1, nd):
+        o_now = jax.lax.ppermute(o_now, axis_name="row", perm=arr_next)
+        runs.insert(0, o_now)
+    built = jnp.concatenate(runs, 1)
+    y1 = jax.lax.axis_index("row")
+    prior = y1 + 1
+    gathered = jnp.roll(built, prior * moved.shape[1], 1)
     gathered = gathered.reshape(panel_count, cycles, tile_size, width)
     partners = [gathered[:, turn_index] for turn_index in range(cycles)]
 

time: 116 us -> 126 us (1.086)
  waiting for transfers between devices: 83.2 us -> 95.3 us
    ppermute x0 -> x7, waiting for transfers between devices: none -> 46.8 us  [body(): o_now = jax.lax.ppermute(o_now, axis_name='row', perm=arr_next)]
    all_gather x1 -> x0, waiting for transfers between devices: 30 us -> none  [body(): gathered = lax.all_gather(moved, 'row', axis=1, tiled=True)]
    all_gather x1, waiting for transfers between devices: 27.9 us -> 23.9 us  [body(): own_tile = lax.all_gather(jacobian, 'col', axis=1, tiled=True)]
    cond x1, local copies, waits for them, and re-layouts: 1.73 us -> 0.14 us  [body(): lax.cond(column_tile <= row_index, product, empty_tile, partners[turn_ind...]
  transfers between devices with their start and end apart: 6 -> 12, of which waited for: 6 -> 12; matrix products, arithmetic and copies ran while one was open for 1% -> 0% of each run, Pallas kernels for 0% -> 0%
where the time goes in v1:
time: 126 us
  waiting for transfers between devices  95.3 us (76%)
  between operations  13.6 us (11%)
  matrix products  7.15 us (6%)
  starting transfers between devices  5.8 us (5%)
  other arithmetic  3.73 us (3%)
    ppermute x7, waiting for transfers between devices, body(): o_now = jax.lax.ppermute(o_now, axis_name='row', perm=arr_next)  46.8 us
    ppermute x4, waiting for transfers between devices, from_partner(): return lax.ppermute(block, axis, route)  24.6 us
    all_gather x1, waiting for transfers between devices, body(): own_tile = lax.all_gather(jacobian, 'col', axis=1, tiled=True)  23.9 us
    dot_general x2, matrix products, product(): jnp.einsum('pak,pbk->ab', own_tile, partner, precision=lax.Precision.HIGH...  7.15 us
    ppermute x4, starting transfers between devices, from_partner(): return lax.ppermute(block, axis, route)  5.72 us
    broadcast_in_dim x1, other arithmetic, body(): return blocks[None, :, None]  2.71 us
  transfers between devices with their start and end apart: 12, of which 12 were waited for; matrix products, arithmetic and copies ran while one was open for 0% of the time, Pallas kernels for 0%

profile of v1, /device:TPU:4, one launch (start us, length us, event | category | flops | bytes accessed | tf_op | source)
XLA Modules:
  0.0 126.2 jit_solution(11866108046878001216)
XLA Ops:
  6.5 1.6 %collective-permute-start = (f32[2,128,256]{2,1,0:T(8,128)}, f32[2,128,256]{2,1,0:T(8,128)S(1)}, u32[]{:S(2)}, u32[]{:S(2)}) collective-permute-start(f32[2,128,256]{2,1,0:T(8,128)} %param.5), channel_id=1, source_target_pairs={{0,1},{1,0},{2,3},{3,2},{4,5},{5,4},{6,7},{7,6},{8,9},{9,8},{10,11... | collective-permute-start | bytes 786440 | tf_op jit(solution)/shard_map/ppermute | solution.py:14
  8.1 6.7 %collective-permute-done = f32[2,128,256]{2,1,0:T(8,128)S(1)} collective-permute-done((f32[2,128,256]{2,1,0:T(8,128)}, f32[2,128,256]{2,1,0:T(8,128)S(1)}, u32[]{:S(2)}, u32[]{:S(2)}) %collective-permute-start) | collective-permute-done | bytes 262176 | tf_op jit(solution)/shard_map/ppermute | solution.py:14
  14.8 0.0 collective-permute-start.1
  14.8 1.5 %collective-permute-done.1 = f32[2,128,256]{2,1,0:T(8,128)S(1)} collective-permute-done((f32[2,128,256]{2,1,0:T(8,128)S(1)}, f32[2,128,256]{2,1,0:T(8,128)S(1)}, u32[]{:S(2)}, u32[]{:S(2)}) %collective-permute-start.1) | collective-permute-done | bytes 262176 | tf_op jit(solution)/shard_map/ppermute | solution.py:14
  16.3 1.0 broadcast_select_fusion
  17.3 2.7 %collective-permute-start.2 = (f32[2,128,256]{2,1,0:T(8,128)S(1)}, f32[2,128,256]{2,1,0:T(8,128)S(1)}, u32[]{:S(2)}, u32[]{:S(2)}) collective-permute-start(f32[2,128,256]{2,1,0:T(8,128)S(1)} %broadcast_select_fusion), channel_id=1, source_target_pairs={{0,2},{2,0},{1,3},{3,1},{4,6},{6,4},{5,7},{7,5},{8,10},{10,8},{9,1... | collective-permute-start | bytes 786440 | tf_op jit(solution)/shard_map/ppermute | solution.py:14
  20.0 11.3 %collective-permute-done.2 = f32[2,128,256]{2,1,0:T(8,128)S(1)} collective-permute-done((f32[2,128,256]{2,1,0:T(8,128)S(1)}, f32[2,128,256]{2,1,0:T(8,128)S(1)}, u32[]{:S(2)}, u32[]{:S(2)}) %collective-permute-start.2) | collective-permute-done | bytes 262176 | tf_op jit(solution)/shard_map/ppermute | solution.py:14
  31.3 1.5 %collective-permute-start.3 = (f32[2,128,256]{2,1,0:T(8,128)S(1)}, f32[2,128,256]{2,1,0:T(8,128)S(1)}, u32[]{:S(2)}, u32[]{:S(2)}) collective-permute-start(f32[2,128,256]{2,1,0:T(8,128)S(1)} %collective-permute-done.2), channel_id=1, source_target_pairs={{0,8},{8,0},{1,9},{9,1},{2,10},{10,2},{3,11},{11,3},{4,12},{12,4},... | collective-permute-start | bytes 786440 | tf_op jit(solution)/shard_map/ppermute | solution.py:14
  32.8 5.1 %collective-permute-done.3 = f32[2,128,256]{2,1,0:T(8,128)S(1)} collective-permute-done((f32[2,128,256]{2,1,0:T(8,128)S(1)}, f32[2,128,256]{2,1,0:T(8,128)S(1)}, u32[]{:S(2)}, u32[]{:S(2)}) %collective-permute-start.3) | collective-permute-done | bytes 262176 | tf_op jit(solution)/shard_map/ppermute | solution.py:14
  37.9 0.1 collective-permute-start.4
  37.9 6.7 %collective-permute-done.4 = f32[2,128,256]{2,1,0:T(8,128)S(1)} collective-permute-done((f32[2,128,256]{2,1,0:T(8,128)S(1)}, f32[2,128,256]{2,1,0:T(8,128)S(1)}, u32[]{:S(2)}, u32[]{:S(2)}) %collective-permute-start.4) | collective-permute-done | bytes 262176 | tf_op jit(solution)/shard_map/ppermute | solution.py:43
  44.6 0.0 collective-permute-start.5
  44.6 6.7 %collective-permute-done.5 = f32[2,128,256]{2,1,0:T(8,128)S(1)} collective-permute-done((f32[2,128,256]{2,1,0:T(8,128)S(1)}, f32[2,128,256]{2,1,0:T(8,128)S(1)}, u32[]{:S(2)}, u32[]{:S(2)}) %collective-permute-start.5) | collective-permute-done | bytes 262176 | tf_op jit(solution)/shard_map/ppermute | solution.py:43
  51.3 0.0 collective-permute-start.6
  51.3 6.7 %collective-permute-done.6 = f32[2,128,256]{2,1,0:T(8,128)S(1)} collective-permute-done((f32[2,128,256]{2,1,0:T(8,128)S(1)}, f32[2,128,256]{2,1,0:T(8,128)S(1)}, u32[]{:S(2)}, u32[]{:S(2)}) %collective-permute-start.6) | collective-permute-done | bytes 262176 | tf_op jit(solution)/shard_map/ppermute | solution.py:43
  58.0 0.0 collective-permute-start.7
  58.0 6.7 %collective-permute-done.7 = f32[2,128,256]{2,1,0:T(8,128)S(1)} collective-permute-done((f32[2,128,256]{2,1,0:T(8,128)S(1)}, f32[2,128,256]{2,1,0:T(8,128)S(1)}, u32[]{:S(2)}, u32[]{:S(2)}) %collective-permute-start.7) | collective-permute-done | bytes 262176 | tf_op jit(solution)/shard_map/ppermute | solution.py:43
  64.7 0.0 collective-permute-start.8
  64.7 6.7 %collective-permute-done.8 = f32[2,128,256]{2,1,0:T(8,128)S(1)} collective-permute-done((f32[2,128,256]{2,1,0:T(8,128)S(1)}, f32[2,128,256]{2,1,0:T(8,128)S(1)}, u32[]{:S(2)}, u32[]{:S(2)}) %collective-permute-start.8) | collective-permute-done | bytes 262176 | tf_op jit(solution)/shard_map/ppermute | solution.py:43
  71.4 0.0 collective-permute-start.9
  71.4 6.7 %collective-permute-done.9 = f32[2,128,256]{2,1,0:T(8,128)S(1)} collective-permute-done((f32[2,128,256]{2,1,0:T(8,128)S(1)}, f32[2,128,256]{2,1,0:T(8,128)S(1)}, u32[]{:S(2)}, u32[]{:S(2)}) %collective-permute-start.9) | collective-permute-done | bytes 262176 | tf_op jit(solution)/shard_map/ppermute | solution.py:43
  78.1 0.0 collective-permute-start.10
  78.1 0.0 all-gather.2.cloned.1.call-update
  78.2 6.6 %collective-permute-done.10 = f32[2,128,256]{2,1,0:T(8,128)S(1)} collective-permute-done((f32[2,128,256]{2,1,0:T(8,128)S(1)}, f32[2,128,256]{2,1,0:T(8,128)S(1)}, u32[]{:S(2)}, u32[]{:S(2)}) %collective-permute-start.10) | collective-permute-done | bytes 262176 | tf_op jit(solution)/shard_map/ppermute | solution.py:43
  85.3 0.1 constant_dynamic-slice_fusion
  85.4 0.1 copy.2
  85.5 23.9 %all-gather.2.cloned.1.call-done = f32[2,512,256]{2,1,0:T(8,128)} async-done(((f32[2,128,256]{2,1,0:T(8,128)}), f32[2,512,256]{2,1,0:T(8,128)}) %all-gather.2.cloned.1.call-update) | async-done | bytes 1048592 | tf_op jit(solution)/shard_map/all_gather | solution.py:28
  109.4 3.1 %conditional.2 = (f32[1,512,512]{2,1,0:T(8,128)S(1)}) conditional(s32[]{:T(128)} %convert_element_type.6, () %tuple.21, (f32[2,2,512,256]{3,2,0,1:T(8,128)S(1)}, f32[2,512,256]{2,1,0:T(8,128)}) %tuple.24), branch_computations={%region_0.1_spmd, %region_1.2_spmd} | conditional | flops 1610612736 | bytes 3145736 | solution.py:62
  109.4 3.1 %convolution_bitcast_fusion = f32[1,512,512]{2,1,0:T(8,128)S(1)} fusion(f32[2,512,256]{2,1,0:T(8,128)} %get-tuple-element.25, f32[2,2,512,256]{3,2,0,1:T(8,128)S(1)} %get-tuple-element.26), kind=kOutput, calls=%fused_computation | convolution fusion | flops 1610612736 | bytes 3145728 | tf_op jit(solution)/shard_map/cond/branch_1_fun/pak,pbk->ab/dot_general | solution.py:53
  112.5 4.1 %conditional.3 = (f32[1,512,512]{2,1,0:T(8,128)}) conditional(s32[]{:T(128)} %convert_element_type.7, () %tuple.23, (f32[2,2,512,256]{3,2,0,1:T(8,128)S(1)}, f32[2,512,256]{2,1,0:T(8,128)}) %tuple.24), branch_computations={%region_2.3_spmd, %region_3.4_spmd} | conditional | flops 1610612736 | bytes 3145736 | solution.py:62
  112.5 4.1 %convolution_bitcast_fusion.1 = f32[1,512,512]{2,1,0:T(8,128)} fusion(f32[2,512,256]{2,1,0:T(8,128)} %get-tuple-element.27, f32[2,2,512,256]{3,2,0,1:T(8,128)S(1)} %get-tuple-element.28), kind=kOutput, calls=%fused_computation.3 | convolution fusion | flops 1610612736 | bytes 3145728 | tf_op jit(solution)/shard_map/cond/branch_1_fun/pak,pbk->ab/dot_general | solution.py:53
  116.6 2.7 %maximum_bitcast_fusion = f32[1,2,1,512,512]{4,3,2,1,0:T(8,128)} fusion(f32[1,512,512]{2,1,0:T(8,128)} %get-tuple-element.34, f32[1,512,512]{2,1,0:T(8,128)S(1)} %get-tuple-element.33), kind=kLoop, calls=%fused_computation.6 | loop fusion | flops 524288 | bytes 4194304 | tf_op jit(solution)/shard_map/broadcast_in_dim | solution.py:65
  (18 shorter events, 0.4 us)
Async XLA Ops:
  6.5 102.9 %all-gather.2.cloned.1.call-start = ((), (), s32[]{:S(2)}) async-start(), calls=%async_computation | async-start | bytes 1310720 | tf_op jit(solution)/shard_map/all_gather | solution.py:28
  6.5 8.3 %collective-permute-start = (f32[2,128,256]{2,1,0:T(8,128)}, f32[2,128,256]{2,1,0:T(8,128)S(1)}, u32[]{:S(2)}, u32[]{:S(2)}) collective-permute-start(f32[2,128,256]{2,1,0:T(8,128)} %param.5), channel_id=1, source_target_pairs={{0,1},{1,0},{2,3},{3,2},{4,5},{5,4},{6,7},{7,6},{8,9},{9,8},{10,11... | collective-permute-start | bytes 786440 | tf_op jit(solution)/shard_map/ppermute | solution.py:14
  14.8 1.5 %collective-permute-start.1 = (f32[2,128,256]{2,1,0:T(8,128)S(1)}, f32[2,128,256]{2,1,0:T(8,128)S(1)}, u32[]{:S(2)}, u32[]{:S(2)}) collective-permute-start(f32[2,128,256]{2,1,0:T(8,128)S(1)} %collective-permute-done), channel_id=1, source_target_pairs={{0,4},{4,0},{1,5},{5,1},{2,6},{6,2},{3,7},{7,3},{8,12},{12,8},{9,1... | collective-permute-start | bytes 786440 | tf_op jit(solution)/shard_map/ppermute | solution.py:14
  17.3 14.0 %collective-permute-start.2 = (f32[2,128,256]{2,1,0:T(8,128)S(1)}, f32[2,128,256]{2,1,0:T(8,128)S(1)}, u32[]{:S(2)}, u32[]{:S(2)}) collective-permute-start(f32[2,128,256]{2,1,0:T(8,128)S(1)} %broadcast_select_fusion), channel_id=1, source_target_pairs={{0,2},{2,0},{1,3},{3,1},{4,6},{6,4},{5,7},{7,5},{8,10},{10,8},{9,1... | collective-permute-start | bytes 786440 | tf_op jit(solution)/shard_map/ppermute | solution.py:14
  31.3 6.5 %collective-permute-start.3 = (f32[2,128,256]{2,1,0:T(8,128)S(1)}, f32[2,128,256]{2,1,0:T(8,128)S(1)}, u32[]{:S(2)}, u32[]{:S(2)}) collective-permute-start(f32[2,128,256]{2,1,0:T(8,128)S(1)} %collective-permute-done.2), channel_id=1, source_target_pairs={{0,8},{8,0},{1,9},{9,1},{2,10},{10,2},{3,11},{11,3},{4,12},{12,4},... | collective-permute-start | bytes 786440 | tf_op jit(solution)/shard_map/ppermute | solution.py:14
  37.9 6.7 %collective-permute-start.4 = (f32[2,128,256]{2,1,0:T(8,128)S(1)}, f32[2,128,256]{2,1,0:T(8,128)S(1)}, u32[]{:S(2)}, u32[]{:S(2)}) collective-permute-start(f32[2,128,256]{2,1,0:T(8,128)S(1)} %broadcast_select_fusion.1), channel_id=1, source_target_pairs={{0,4},{4,8},{8,12},{12,16},{16,20},{20,24},{24,28},{28,0},{1,5},{5... | collective-permute-start | bytes 786440 | tf_op jit(solution)/shard_map/ppermute | solution.py:43
  44.6 6.7 %collective-permute-start.5 = (f32[2,128,256]{2,1,0:T(8,128)S(1)}, f32[2,128,256]{2,1,0:T(8,128)S(1)}, u32[]{:S(2)}, u32[]{:S(2)}) collective-permute-start(f32[2,128,256]{2,1,0:T(8,128)S(1)} %collective-permute-done.4), channel_id=1, source_target_pairs={{0,4},{4,8},{8,12},{12,16},{16,20},{20,24},{24,28},{28,0},{1,5},{5... | collective-permute-start | bytes 786440 | tf_op jit(solution)/shard_map/ppermute | solution.py:43
  51.3 6.7 %collective-permute-start.6 = (f32[2,128,256]{2,1,0:T(8,128)S(1)}, f32[2,128,256]{2,1,0:T(8,128)S(1)}, u32[]{:S(2)}, u32[]{:S(2)}) collective-permute-start(f32[2,128,256]{2,1,0:T(8,128)S(1)} %collective-permute-done.5), channel_id=1, source_target_pairs={{0,4},{4,8},{8,12},{12,16},{16,20},{20,24},{24,28},{28,0},{1,5},{5... | collective-permute-start | bytes 786440 | tf_op jit(solution)/shard_map/ppermute | solution.py:43
  58.0 6.7 %collective-permute-start.7 = (f32[2,128,256]{2,1,0:T(8,128)S(1)}, f32[2,128,256]{2,1,0:T(8,128)S(1)}, u32[]{:S(2)}, u32[]{:S(2)}) collective-permute-start(f32[2,128,256]{2,1,0:T(8,128)S(1)} %collective-permute-done.6), channel_id=1, source_target_pairs={{0,4},{4,8},{8,12},{12,16},{16,20},{20,24},{24,28},{28,0},{1,5},{5... | collective-permute-start | bytes 786440 | tf_op jit(solution)/shard_map/ppermute | solution.py:43
  64.7 6.7 %collective-permute-start.8 = (f32[2,128,256]{2,1,0:T(8,128)S(1)}, f32[2,128,256]{2,1,0:T(8,128)S(1)}, u32[]{:S(2)}, u32[]{:S(2)}) collective-permute-start(f32[2,128,256]{2,1,0:T(8,128)S(1)} %collective-permute-done.7), channel_id=1, source_target_pairs={{0,4},{4,8},{8,12},{12,16},{16,20},{20,24},{24,28},{28,0},{1,5},{5... | collective-permute-start | bytes 786440 | tf_op jit(solution)/shard_map/ppermute | solution.py:43
  71.4 6.7 %collective-permute-start.9 = (f32[2,128,256]{2,1,0:T(8,128)S(1)}, f32[2,128,256]{2,1,0:T(8,128)S(1)}, u32[]{:S(2)}, u32[]{:S(2)}) collective-permute-start(f32[2,128,256]{2,1,0:T(8,128)S(1)} %collective-permute-done.8), channel_id=1, source_target_pairs={{0,4},{4,8},{8,12},{12,16},{16,20},{20,24},{24,28},{28,0},{1,5},{5... | collective-permute-start | bytes 786440 | tf_op jit(solution)/shard_map/ppermute | solution.py:43
  78.1 6.7 %collective-permute-start.10 = (f32[2,128,256]{2,1,0:T(8,128)S(1)}, f32[2,128,256]{2,1,0:T(8,128)S(1)}, u32[]{:S(2)}, u32[]{:S(2)}) collective-permute-start(f32[2,128,256]{2,1,0:T(8,128)S(1)} %collective-permute-done.9), channel_id=1, source_target_pairs={{0,4},{4,8},{8,12},{12,16},{16,20},{20,24},{24,28},{28,0},{1,5},{5... | collective-permute-start | bytes 786440 | tf_op jit(solution)/shard_map/ppermute | solution.py:43
Sparse Core Ops, SparseCore 0:
  78.3 31.1 all-gather.1
